TPU v7x, 128 devices: a whole 4x4x4 slice. The times are simulated.
128 devices in a mesh: sec: 64 (over x, y, z), node: 2 (over core).
Axes of the slice: x: 4, y: 4, z: 4, core: 2. Of those that a mesh axis runs over, the one named last changes fastest.
Arguments:
- env_blocks: bfloat16 [2, 24576, 128, 128], P('node', 'sec'), may hold values from -10 to 10, as said below
- iso_blocks: bfloat16 [2, 24576, 128, 128], P('node', 'sec'), may hold values from -6 to 6
- joined_sector: int32 [2, 24576], P('node', 'sec'), may hold values from 0 to 63, as said below
- owner_map: int32 [2, 64], P('node'), may hold values from 0 to 63, each once within a row
- live_pairs: int32 [2, 64], P('node', 'sec'), may hold values from 1 to 384, as said below
Outputs:
- environment: float32 [2, 64, 128, 128], P('node', 'sec')
Inputs may be any that keep to these rules, and one draw needn't show every extreme that they name: `env_blocks`: each block is symmetric. `joined_sector`: slot p belongs to tree node k = p // 3072 of its group, and its sector is one of that node's sectors k * 8 to k * 8 + 7. `owner_map`: each row names every index once. `live_pairs`: in every group some index of sec has all 384 slots live.
All inputs are finite; a program needn't handle non-finite values.
Results may differ from a plain program's by a relative error of at most 0.0003.
Values sent between devices are 32-bit elements; how exact they have to be, the bound alone decides.
A program may use at most 128 MiB of HBM per device.

v0:
```python
import jax
import jax.numpy as jnp
from jax import lax
from jax.sharding import Mesh
from jax.sharding import PartitionSpec as P

SEC = ("sec_0", "sec_1", "sec_2")
SEC_NODE = ("sec_0", "sec_1", "sec_2", "node")


pair_group = 32


def cut_along(shard, dim, length):
    shape = shard.shape
    blocks = shard.reshape(*shape[:dim], length, shape[dim] // length, *shape[dim + 1 :])
    return jnp.moveaxis(blocks, dim, 0)


def sum_at_owner(shard, axis, dim):
    length = lax.axis_size(axis)
    blocks = lax.all_to_all(cut_along(shard, dim, length), axis, 0, 0, tiled=True)
    return jnp.sum(blocks, axis=0)


def by_axis(shard, axes):
    for axis in axes:
        shard = lax.psum(shard, axis)
    return shard


def body(env_blocks, iso_blocks, joined_sector, owner_map, live_pairs):
    pairs_here = env_blocks.shape[1]
    sector_width = iso_blocks.shape[3]
    half_width = sector_width // 2
    sectors = lax.axis_size(SEC)
    sector_ids = jnp.arange(sectors, dtype=jnp.int32)
    matches = joined_sector[0][:, None] == sector_ids[None, :]
    targets = jnp.sum(jnp.where(matches, owner_map[0][None, :], 0), axis=1)
    living = jnp.arange(pairs_here, dtype=jnp.int32) < live_pairs[0, 0]

    def add_group(turn_index, partial_value):
        first_pair = turn_index * pair_group
        blocks = lax.dynamic_slice_in_dim(env_blocks[0], first_pair, pair_group, 0)
        weights = lax.dynamic_slice_in_dim(iso_blocks[0], first_pair, pair_group, 0)
        group_targets = lax.dynamic_slice_in_dim(targets, first_pair, pair_group, 0)
        group_live = lax.dynamic_slice_in_dim(living, first_pair, pair_group, 0)
        product = jnp.einsum(
            "prk,pkc->prc", blocks, weights, preferred_element_type=jnp.float32
        ).astype(jnp.bfloat16)
        sandwich = jnp.einsum("prc,prd->pcd", weights, product, preferred_element_type=jnp.float32)
        selector = ((group_targets[:, None] == sector_ids[None, :]) & group_live[:, None]).astype(
            jnp.float32
        )
        flat_terms = sandwich.reshape(pair_group, sector_width * sector_width)
        added = lax.dot_general(
            selector,
            flat_terms,
            (((0,), (0,)), ((), ())),
            precision=lax.Precision.HIGHEST,
            preferred_element_type=jnp.float32,
        )
        return partial_value + added

    zero_sums = jnp.zeros((sectors, sector_width * sector_width), jnp.float32)
    turn_total = pairs_here // pair_group
    partial_value = lax.fori_loop(0, turn_total, add_group, zero_sums).reshape(
        sectors, sector_width, sector_width
    )
    upper_left = partial_value[:, :half_width, :half_width]
    upper_right = partial_value[:, :half_width, half_width:]
    lower_right = partial_value[:, half_width:, half_width:]
    corners = jnp.triu(upper_left) + jnp.tril(jnp.swapaxes(lower_right, 1, 2), -1)
    diagonal_row = jnp.diagonal(lower_right, axis1=1, axis2=2)[:, None, :]
    packed = jnp.concatenate((corners, upper_right, diagonal_row), axis=1)
    summed = sum_at_owner(packed, SEC, 0)[0]
    corners_sum = summed[:half_width]
    right_sum = summed[half_width : 2 * half_width]
    diagonal_sum = summed[2 * half_width]
    left_block = jnp.triu(corners_sum) + jnp.triu(corners_sum, 1).T
    lower_upper = jnp.tril(corners_sum, -1).T + jnp.diag(diagonal_sum)
    right_block = lower_upper + jnp.triu(lower_upper, 1).T
    top_rows = jnp.concatenate((left_block, right_sum), axis=1)
    bottom_rows = jnp.concatenate((right_sum.T, right_block), axis=1)
    hermitian = jnp.concatenate((top_rows, bottom_rows), axis=0)
    squares = jnp.sum(hermitian * hermitian)
    grand_total = by_axis(squares, SEC_NODE)
    entries = sectors * lax.axis_size("node") * sector_width * sector_width
    factor = lax.rsqrt(grand_total / entries + 1e-06)
    return (hermitian * factor)[None, None]


def solution(mesh):
    split = Mesh(
        mesh.devices.reshape(4, 4, 4, mesh.shape["node"]), ("sec_0", "sec_1", "sec_2", "node")
    )
    placed = (
        P("node", SEC, None, None),
        P("node", SEC, None, None),
        P("node", SEC),
        P("node", None),
        P("node", SEC),
    )
    return jax.shard_map(
        body, mesh=split, in_specs=placed, out_specs=P("node", SEC, None, None), check_vma=False
    )
```

profile of v0, /device:TPU:1, one launch (start us, length us, event | category | flops | bytes accessed | tf_op | source)
XLA Modules:
  0.0 255.1 jit_solution(2081290549324022647)
XLA Ops:
  0.0 0.7 reduce.1
  1.4 0.7 select_reduce_fusion
  2.1 121.4 %while.14 = (s32[]{:T(128)}, f32[64,16384]{1,0:T(8,128)}, s32[384]{0:T(512)S(1)}, pred[384]{0:T(512)(128)(4,1)S(1)}, bf16[1,384,128,128]{3,2,1,0:T(8,128)(2,1)},...) while((s32[]{:T(128)}, f32[64,16384]{1,0:T(8,128)}, ...), condition=%wide.region_2.3_spmd.clone, body=%wide.region_1.2_spmd.clone.sunk | while | flops 673714176 | bytes 15730821 | solution.py:67
  2.1 2.6 %fusion.36 = f32[32,128,128]{2,1,0:T(8,128)S(1)} fusion(bf16[1,384,128,128]{3,2,1,0:T(8,128)(2,1)} %get-tuple-element.248, s32[]{:T(128)S(6)} %select_n.72, bf16[1,384,128,128]{3,2,1,0:T(8,128)(2,1)} %get-tuple-element.247), kind=kOutput, calls=%fused_computation.6.clone.1 | convolution fusion | flops 268959744 | bytes 5244416 | tf_op jit(solution)/shard_map/while/body/eval_jaxpr/prc,prd->pcd/dot_general | solution.py:51
  4.9 5.3 %convolution_add_fusion.2 = f32[64,16384]{1,0:T(8,128)} fusion(f32[64,16384]{1,0:T(8,128)} %get-tuple-element.234, f32[4,8,128,128]{3,2,1,0:T(8,128)S(1)} %bitcast.64, pred[]{:T(512)S(6)} %compare.3, s32[32]{0:T(128)S(1)} %dynamic_slice.54, pred[32]{0:T(512)(128)(4,1)S(1)} %dynamic_slice.55), kind=kOutput, calls=%fused_computation.2.clone.1 | convolution fusion | flops 404754432 | bytes 10485921 | tf_op jit(solution)/shard_map/while/body/eval_jaxpr/dot_general | solution.py:56
  10.2 2.6 %fusion.36 = f32[32,128,128]{2,1,0:T(8,128)S(1)} fusion(bf16[1,384,128,128]{3,2,1,0:T(8,128)(2,1)} %get-tuple-element.248, s32[]{:T(128)S(6)} %select_n.72, bf16[1,384,128,128]{3,2,1,0:T(8,128)(2,1)} %get-tuple-element.247), kind=kOutput, calls=%fused_computation.6.clone.1 | convolution fusion | flops 268959744 | bytes 5244416 | tf_op jit(solution)/shard_map/while/body/eval_jaxpr/prc,prd->pcd/dot_general | solution.py:51
  13.0 7.5 %convolution_add_fusion.2 = f32[64,16384]{1,0:T(8,128)} fusion(f32[64,16384]{1,0:T(8,128)} %get-tuple-element.234, f32[4,8,128,128]{3,2,1,0:T(8,128)S(1)} %bitcast.64, pred[]{:T(512)S(6)} %compare.3, s32[32]{0:T(128)S(1)} %dynamic_slice.54, pred[32]{0:T(512)(128)(4,1)S(1)} %dynamic_slice.55), kind=kOutput, calls=%fused_computation.2.clone.1 | convolution fusion | flops 404754432 | bytes 10485921 | tf_op jit(solution)/shard_map/while/body/eval_jaxpr/dot_general | solution.py:56
  20.5 2.6 %fusion.36 = f32[32,128,128]{2,1,0:T(8,128)S(1)} fusion(bf16[1,384,128,128]{3,2,1,0:T(8,128)(2,1)} %get-tuple-element.248, s32[]{:T(128)S(6)} %select_n.72, bf16[1,384,128,128]{3,2,1,0:T(8,128)(2,1)} %get-tuple-element.247), kind=kOutput, calls=%fused_computation.6.clone.1 | convolution fusion | flops 268959744 | bytes 5244416 | tf_op jit(solution)/shard_map/while/body/eval_jaxpr/prc,prd->pcd/dot_general | solution.py:51
  23.3 7.5 %convolution_add_fusion.2 = f32[64,16384]{1,0:T(8,128)} fusion(f32[64,16384]{1,0:T(8,128)} %get-tuple-element.234, f32[4,8,128,128]{3,2,1,0:T(8,128)S(1)} %bitcast.64, pred[]{:T(512)S(6)} %compare.3, s32[32]{0:T(128)S(1)} %dynamic_slice.54, pred[32]{0:T(512)(128)(4,1)S(1)} %dynamic_slice.55), kind=kOutput, calls=%fused_computation.2.clone.1 | convolution fusion | flops 404754432 | bytes 10485921 | tf_op jit(solution)/shard_map/while/body/eval_jaxpr/dot_general | solution.py:56
  30.8 2.6 %fusion.36 = f32[32,128,128]{2,1,0:T(8,128)S(1)} fusion(bf16[1,384,128,128]{3,2,1,0:T(8,128)(2,1)} %get-tuple-element.248, s32[]{:T(128)S(6)} %select_n.72, bf16[1,384,128,128]{3,2,1,0:T(8,128)(2,1)} %get-tuple-element.247), kind=kOutput, calls=%fused_computation.6.clone.1 | convolution fusion | flops 268959744 | bytes 5244416 | tf_op jit(solution)/shard_map/while/body/eval_jaxpr/prc,prd->pcd/dot_general | solution.py:51
  33.5 7.5 %convolution_add_fusion.2 = f32[64,16384]{1,0:T(8,128)} fusion(f32[64,16384]{1,0:T(8,128)} %get-tuple-element.234, f32[4,8,128,128]{3,2,1,0:T(8,128)S(1)} %bitcast.64, pred[]{:T(512)S(6)} %compare.3, s32[32]{0:T(128)S(1)} %dynamic_slice.54, pred[32]{0:T(512)(128)(4,1)S(1)} %dynamic_slice.55), kind=kOutput, calls=%fused_computation.2.clone.1 | convolution fusion | flops 404754432 | bytes 10485921 | tf_op jit(solution)/shard_map/while/body/eval_jaxpr/dot_general | solution.py:56
  41.0 2.6 %fusion.36 = f32[32,128,128]{2,1,0:T(8,128)S(1)} fusion(bf16[1,384,128,128]{3,2,1,0:T(8,128)(2,1)} %get-tuple-element.248, s32[]{:T(128)S(6)} %select_n.72, bf16[1,384,128,128]{3,2,1,0:T(8,128)(2,1)} %get-tuple-element.247), kind=kOutput, calls=%fused_computation.6.clone.1 | convolution fusion | flops 268959744 | bytes 5244416 | tf_op jit(solution)/shard_map/while/body/eval_jaxpr/prc,prd->pcd/dot_general | solution.py:51
  43.8 7.5 %convolution_add_fusion.2 = f32[64,16384]{1,0:T(8,128)} fusion(f32[64,16384]{1,0:T(8,128)} %get-tuple-element.234, f32[4,8,128,128]{3,2,1,0:T(8,128)S(1)} %bitcast.64, pred[]{:T(512)S(6)} %compare.3, s32[32]{0:T(128)S(1)} %dynamic_slice.54, pred[32]{0:T(512)(128)(4,1)S(1)} %dynamic_slice.55), kind=kOutput, calls=%fused_computation.2.clone.1 | convolution fusion | flops 404754432 | bytes 10485921 | tf_op jit(solution)/shard_map/while/body/eval_jaxpr/dot_general | solution.py:56
  51.3 2.6 %fusion.36 = f32[32,128,128]{2,1,0:T(8,128)S(1)} fusion(bf16[1,384,128,128]{3,2,1,0:T(8,128)(2,1)} %get-tuple-element.248, s32[]{:T(128)S(6)} %select_n.72, bf16[1,384,128,128]{3,2,1,0:T(8,128)(2,1)} %get-tuple-element.247), kind=kOutput, calls=%fused_computation.6.clone.1 | convolution fusion | flops 268959744 | bytes 5244416 | tf_op jit(solution)/shard_map/while/body/eval_jaxpr/prc,prd->pcd/dot_general | solution.py:51
  54.1 7.5 %convolution_add_fusion.2 = f32[64,16384]{1,0:T(8,128)} fusion(f32[64,16384]{1,0:T(8,128)} %get-tuple-element.234, f32[4,8,128,128]{3,2,1,0:T(8,128)S(1)} %bitcast.64, pred[]{:T(512)S(6)} %compare.3, s32[32]{0:T(128)S(1)} %dynamic_slice.54, pred[32]{0:T(512)(128)(4,1)S(1)} %dynamic_slice.55), kind=kOutput, calls=%fused_computation.2.clone.1 | convolution fusion | flops 404754432 | bytes 10485921 | tf_op jit(solution)/shard_map/while/body/eval_jaxpr/dot_general | solution.py:56
  61.6 2.8 %fusion.36 = f32[32,128,128]{2,1,0:T(8,128)S(1)} fusion(bf16[1,384,128,128]{3,2,1,0:T(8,128)(2,1)} %get-tuple-element.248, s32[]{:T(128)S(6)} %select_n.72, bf16[1,384,128,128]{3,2,1,0:T(8,128)(2,1)} %get-tuple-element.247), kind=kOutput, calls=%fused_computation.6.clone.1 | convolution fusion | flops 268959744 | bytes 5244416 | tf_op jit(solution)/shard_map/while/body/eval_jaxpr/prc,prd->pcd/dot_general | solution.py:51
  64.6 7.5 %convolution_add_fusion.2 = f32[64,16384]{1,0:T(8,128)} fusion(f32[64,16384]{1,0:T(8,128)} %get-tuple-element.234, f32[4,8,128,128]{3,2,1,0:T(8,128)S(1)} %bitcast.64, pred[]{:T(512)S(6)} %compare.3, s32[32]{0:T(128)S(1)} %dynamic_slice.54, pred[32]{0:T(512)(128)(4,1)S(1)} %dynamic_slice.55), kind=kOutput, calls=%fused_computation.2.clone.1 | convolution fusion | flops 404754432 | bytes 10485921 | tf_op jit(solution)/shard_map/while/body/eval_jaxpr/dot_general | solution.py:56
  72.1 2.6 %fusion.36 = f32[32,128,128]{2,1,0:T(8,128)S(1)} fusion(bf16[1,384,128,128]{3,2,1,0:T(8,128)(2,1)} %get-tuple-element.248, s32[]{:T(128)S(6)} %select_n.72, bf16[1,384,128,128]{3,2,1,0:T(8,128)(2,1)} %get-tuple-element.247), kind=kOutput, calls=%fused_computation.6.clone.1 | convolution fusion | flops 268959744 | bytes 5244416 | tf_op jit(solution)/shard_map/while/body/eval_jaxpr/prc,prd->pcd/dot_general | solution.py:51
  74.9 7.5 %convolution_add_fusion.2 = f32[64,16384]{1,0:T(8,128)} fusion(f32[64,16384]{1,0:T(8,128)} %get-tuple-element.234, f32[4,8,128,128]{3,2,1,0:T(8,128)S(1)} %bitcast.64, pred[]{:T(512)S(6)} %compare.3, s32[32]{0:T(128)S(1)} %dynamic_slice.54, pred[32]{0:T(512)(128)(4,1)S(1)} %dynamic_slice.55), kind=kOutput, calls=%fused_computation.2.clone.1 | convolution fusion | flops 404754432 | bytes 10485921 | tf_op jit(solution)/shard_map/while/body/eval_jaxpr/dot_general | solution.py:56
  82.4 2.6 %fusion.36 = f32[32,128,128]{2,1,0:T(8,128)S(1)} fusion(bf16[1,384,128,128]{3,2,1,0:T(8,128)(2,1)} %get-tuple-element.248, s32[]{:T(128)S(6)} %select_n.72, bf16[1,384,128,128]{3,2,1,0:T(8,128)(2,1)} %get-tuple-element.247), kind=kOutput, calls=%fused_computation.6.clone.1 | convolution fusion | flops 268959744 | bytes 5244416 | tf_op jit(solution)/shard_map/while/body/eval_jaxpr/prc,prd->pcd/dot_general | solution.py:51
  85.2 7.5 %convolution_add_fusion.2 = f32[64,16384]{1,0:T(8,128)} fusion(f32[64,16384]{1,0:T(8,128)} %get-tuple-element.234, f32[4,8,128,128]{3,2,1,0:T(8,128)S(1)} %bitcast.64, pred[]{:T(512)S(6)} %compare.3, s32[32]{0:T(128)S(1)} %dynamic_slice.54, pred[32]{0:T(512)(128)(4,1)S(1)} %dynamic_slice.55), kind=kOutput, calls=%fused_computation.2.clone.1 | convolution fusion | flops 404754432 | bytes 10485921 | tf_op jit(solution)/shard_map/while/body/eval_jaxpr/dot_general | solution.py:56
  92.7 2.6 %fusion.36 = f32[32,128,128]{2,1,0:T(8,128)S(1)} fusion(bf16[1,384,128,128]{3,2,1,0:T(8,128)(2,1)} %get-tuple-element.248, s32[]{:T(128)S(6)} %select_n.72, bf16[1,384,128,128]{3,2,1,0:T(8,128)(2,1)} %get-tuple-element.247), kind=kOutput, calls=%fused_computation.6.clone.1 | convolution fusion | flops 268959744 | bytes 5244416 | tf_op jit(solution)/shard_map/while/body/eval_jaxpr/prc,prd->pcd/dot_general | solution.py:51
  95.4 7.5 %convolution_add_fusion.2 = f32[64,16384]{1,0:T(8,128)} fusion(f32[64,16384]{1,0:T(8,128)} %get-tuple-element.234, f32[4,8,128,128]{3,2,1,0:T(8,128)S(1)} %bitcast.64, pred[]{:T(512)S(6)} %compare.3, s32[32]{0:T(128)S(1)} %dynamic_slice.54, pred[32]{0:T(512)(128)(4,1)S(1)} %dynamic_slice.55), kind=kOutput, calls=%fused_computation.2.clone.1 | convolution fusion | flops 404754432 | bytes 10485921 | tf_op jit(solution)/shard_map/while/body/eval_jaxpr/dot_general | solution.py:56
  102.9 2.7 %fusion.36 = f32[32,128,128]{2,1,0:T(8,128)S(1)} fusion(bf16[1,384,128,128]{3,2,1,0:T(8,128)(2,1)} %get-tuple-element.248, s32[]{:T(128)S(6)} %select_n.72, bf16[1,384,128,128]{3,2,1,0:T(8,128)(2,1)} %get-tuple-element.247), kind=kOutput, calls=%fused_computation.6.clone.1 | convolution fusion | flops 268959744 | bytes 5244416 | tf_op jit(solution)/shard_map/while/body/eval_jaxpr/prc,prd->pcd/dot_general | solution.py:51
  105.8 7.5 %convolution_add_fusion.2 = f32[64,16384]{1,0:T(8,128)} fusion(f32[64,16384]{1,0:T(8,128)} %get-tuple-element.234, f32[4,8,128,128]{3,2,1,0:T(8,128)S(1)} %bitcast.64, pred[]{:T(512)S(6)} %compare.3, s32[32]{0:T(128)S(1)} %dynamic_slice.54, pred[32]{0:T(512)(128)(4,1)S(1)} %dynamic_slice.55), kind=kOutput, calls=%fused_computation.2.clone.1 | convolution fusion | flops 404754432 | bytes 10485921 | tf_op jit(solution)/shard_map/while/body/eval_jaxpr/dot_general | solution.py:56
  113.3 2.6 %fusion.36 = f32[32,128,128]{2,1,0:T(8,128)S(1)} fusion(bf16[1,384,128,128]{3,2,1,0:T(8,128)(2,1)} %get-tuple-element.248, s32[]{:T(128)S(6)} %select_n.72, bf16[1,384,128,128]{3,2,1,0:T(8,128)(2,1)} %get-tuple-element.247), kind=kOutput, calls=%fused_computation.6.clone.1 | convolution fusion | flops 268959744 | bytes 5244416 | tf_op jit(solution)/shard_map/while/body/eval_jaxpr/prc,prd->pcd/dot_general | solution.py:51
  116.1 7.5 %convolution_add_fusion.2 = f32[64,16384]{1,0:T(8,128)} fusion(f32[64,16384]{1,0:T(8,128)} %get-tuple-element.234, f32[4,8,128,128]{3,2,1,0:T(8,128)S(1)} %bitcast.64, pred[]{:T(512)S(6)} %compare.3, s32[32]{0:T(128)S(1)} %dynamic_slice.54, pred[32]{0:T(512)(128)(4,1)S(1)} %dynamic_slice.55), kind=kOutput, calls=%fused_computation.2.clone.1 | convolution fusion | flops 404754432 | bytes 10485921 | tf_op jit(solution)/shard_map/while/body/eval_jaxpr/dot_general | solution.py:56
  123.6 2.9 %copy.65 = f32[8,8,128,128]{3,2,1,0:T(8,128)S(1)} copy(f32[8,8,128,128]{3,1,2,0:T(8,128)} %bitcast.65) | data formatting | bytes 8388608
  126.5 3.8 %fusion.24 = (f32[64,64,64]{2,1,0:T(8,128)}, f32[64,64,64]{2,1,0:T(8,128)}, f32[64,64,64]{2,1,0:T(8,128)}) fusion(f32[64,128,128]{2,1,0:T(8,128)S(1)} %bitcast.66), kind=kLoop, calls=%fused_computation.43 | loop fusion | bytes 6291456 | tf_op jit(solution)/shard_map/slice | solution.py:70
  130.3 2.4 copy.62
  132.7 4.2 %copy.61 = f32[64,64,64]{0,1,2:T(8,128)} copy(f32[64,64,64]{2,1,0:T(8,128)} %get-tuple-element.177) | data formatting | bytes 2097152
  136.8 4.2 %copy.63 = f32[64,64,64]{0,1,2:T(8,128)} copy(f32[64,64,64]{2,1,0:T(8,128)} %get-tuple-element.178) | data formatting | bytes 2097152
  141.0 0.9 gather_fusion
  141.9 2.1 fusion.19
  144.0 0.1 copy-done
  144.1 2.4 maximum_bitcast_fusion
  146.5 6.4 %copy.53 = f32[64,1,129,64]{2,3,1,0:T(8,128)} copy(f32[64,1,129,64]{0,2,3,1:T(8,128)} %maximum_bitcast_fusion) | data formatting | bytes 4227072 | tf_op jit(solution)/shard_map/reshape | solution.py:16
  152.9 62.3 %all_to_all.5 = f32[64,1,129,64]{2,3,1,0:T(8,128)} all-to-all(f32[64,1,129,64]{2,3,1,0:T(8,128)} %copy.53), channel_id=1, replica_groups=mesh['sec_0'=4,'sec_1'=4,'sec_2'=4,'node'=2] {'sec_0','sec_1','sec_2'}, dimensions={0} | all-to-all | bytes 4227072 | tf_op jit(solution)/shard_map/all_to_all | solution.py:22
  215.2 2.5 reduce_sum.30
  217.7 0.1 slice_reduce_fusion
  217.9 0.1 fusion.21
  218.1 0.1 copy.55
  218.3 0.7 fusion.20
  219.0 7.3 %psum.28 = f32[]{:T(128)} all-reduce(f32[]{:T(128)} %fusion.20), channel_id=1, replica_groups=mesh['sec_0'=4,'sec_1'=4,'sec_2'=4,'node'=2] {'sec_0'}, use_global_device_ids=true, to_apply=%region_5.6 | all-reduce | flops 1 | bytes 8 | tf_op jit(solution)/shard_map/psum | solution.py:28
  226.3 10.5 %psum.29 = f32[]{:T(128)} all-reduce(f32[]{:T(128)} %psum.28), channel_id=1, replica_groups=mesh['sec_0'=4,'sec_1'=4,'sec_2'=4,'node'=2] {'sec_1'}, use_global_device_ids=true, to_apply=%region_6.7 | all-reduce | flops 1 | bytes 8 | tf_op jit(solution)/shard_map/psum | solution.py:28
  236.8 7.6 %psum.30 = f32[]{:T(128)} all-reduce(f32[]{:T(128)} %psum.29), channel_id=1, replica_groups=mesh['sec_0'=4,'sec_1'=4,'sec_2'=4,'node'=2] {'sec_2'}, use_global_device_ids=true, to_apply=%region_7.8 | all-reduce | flops 1 | bytes 8 | tf_op jit(solution)/shard_map/psum | solution.py:28
  244.5 9.3 %psum.31 = f32[]{:T(128)} all-reduce(f32[]{:T(128)} %psum.30), channel_id=1, replica_groups=mesh['sec_0'=4,'sec_1'=4,'sec_2'=4,'node'=2] {'node'}, use_global_device_ids=true, to_apply=%region_8.9 | all-reduce | flops 1 | bytes 8 | tf_op jit(solution)/shard_map/psum | solution.py:28
  254.5 0.6 maximum_multiply_fusion
  (37 shorter events, 2.3 us)
Async XLA Ops:
  141.9 2.2 copy-start
where the time goes:
time: 256 us; the launch traced here: 255 us
  matrix products  119 us (46%)
  blocking collectives  97 us (38%)
  local copies, waits for them, and re-layouts  27.1 us (11%)
  other arithmetic  10 us (4%)
    dot_general x12, matrix products, add_group(): lax.dot_general(selector, flat_terms, (((0,), (0,)), ((), ())), precision...  87.8 us
    all_to_all x1, blocking collectives, sum_at_owner(): lax.all_to_all(cut_along(shard, dim, length), axis, 0, 0, tiled=True)  62.3 us
    psum x4, blocking collectives, by_axis(): shard = lax.psum(shard, axis)  34.7 us
    dot_general x12, matrix products, add_group(): jnp.einsum('prc,prd->pcd', weights, product, preferred_element_type=jnp.f...  31.6 us
    unnamed x6, local copies, waits for them, and re-layouts  13.7 us
    reshape x1, local copies, waits for them, and re-layouts, cut_along(): shard.reshape(*shape[:dim], length, shape[dim] // length, *shape[dim + 1:])  6.38 us

commit v1 on v0

v1 whole, which is shorter than its diff:
```python
import functools

import jax
import jax.numpy as jnp
from jax import lax
from jax.experimental import pallas as pl
from jax.experimental.pallas import tpu as pltpu
from jax.sharding import PartitionSpec as P

MESH = pl.DeviceIdType.MESH
NODE_SECTORS = 8
CHUNK = 16
PAIRS = CHUNK // 2
DEPTH = PAIRS // 2
ROWS = 72
TOP = 40


def pack_rows(full):
    lane = lax.broadcasted_iota(jnp.int32, (16, 128), 1)
    rows = [full[112:128]]
    for low in range(3):
        high = 6 - low
        width = 16 * (high + 1)
        short = pltpu.roll(full[16 * low : 16 * low + 16], width, 1)
        rows.append(jnp.where(lane < width, full[16 * high : 16 * high + 16], short))
    rows.append(jnp.where(lane[:8] < 64, full[48:56], pltpu.roll(full[56:64], 64, 1)))
    return jnp.concatenate(rows, axis=0)


def unpack_rows(packed):
    blocks = [None] * 8
    blocks[7] = packed[0:16]
    for low in range(3):
        high = 6 - low
        width = 16 * (high + 1)
        both = packed[16 + 16 * low : 32 + 16 * low]
        blocks[high] = both
        blocks[low] = pltpu.roll(both, 128 - width, 1)
    blocks[3] = jnp.concatenate((packed[64:72], pltpu.roll(packed[64:72], 64, 1)), axis=0)
    return jnp.concatenate(blocks, axis=0)


def local_kernel(
    live_ref, sector_ref, owner_ref, env_ref, iso_ref, parts_ref, source_ref,
    env_buf, iso_buf, sums_0, sums_1, sums_2, sums_3, env_sem, iso_sem,
):
    live = live_ref[0, 0]
    chunks = (live + CHUNK - 1) // CHUNK
    sums = (sums_0, sums_1, sums_2, sums_3)

    def copies(c):
        first = pl.multiple_of(c * CHUNK, CHUNK)
        span = pl.ds(first, CHUNK)
        return (
            pltpu.make_async_copy(iso_ref.at[0, span], iso_buf.at[span], iso_sem.at[c]),
            pltpu.make_async_copy(env_ref.at[0, span], env_buf.at[span], env_sem.at[c]),
        )

    def start(c, carry):
        for copy in copies(c):
            copy.start()
        return carry

    lax.fori_loop(0, chunks, start, 0)

    def invert(sector, carry):
        source_ref[0, owner_ref[0, sector]] = sector
        return carry

    lax.fori_loop(0, owner_ref.shape[1], invert, 0)

    def clear(sector, carry):
        for ref in sums:
            ref[sector] = jnp.zeros((128, 128), jnp.float32)
        return carry

    lax.fori_loop(0, NODE_SECTORS + 1, clear, 0)

    def await_chunk(c):
        for copy in copies(c):
            copy.wait()

    def target(slot):
        return jnp.where(slot < live, lax.rem(sector_ref[0, slot], NODE_SECTORS), NODE_SECTORS)

    def stacked(c, pair):
        first = c * CHUNK + 2 * pair
        none = jnp.zeros((128, 128), jnp.bfloat16)
        top = jnp.concatenate((iso_buf[first], none), axis=1)
        bottom = jnp.concatenate((none, iso_buf[first + 1]), axis=1)
        return jnp.concatenate((top, bottom), axis=0)

    def run(z_acc, y_acc):
        def first_stage(c, pair):
            mxu, place = pair % 2, pair // 2
            first = c * CHUNK + 2 * pair
            pltpu.matmul_push_rhs(stacked(c, pair), staging_register=0, mxu_index=mxu)
            side = jnp.concatenate((env_buf[first], env_buf[first + 1]), axis=1)
            pltpu.matmul_acc_lhs(z_acc[mxu][place], side, load_staged_rhs=0)

        def turned(pair):
            mxu, place = pair % 2, pair // 2
            z = pltpu.matmul_pop(z_acc[mxu][place]).astype(jnp.bfloat16)
            return jnp.concatenate((z[:, :128].T, z[:, 128:].T), axis=1)

        def second_stage(c, pair, side):
            mxu, place = pair % 2, pair // 2
            pltpu.matmul_push_rhs(stacked(c, pair), staging_register=1, mxu_index=mxu)
            pltpu.matmul_acc_lhs(y_acc[mxu][place], side, load_staged_rhs=1)

        def add(c, pair, drop):
            mxu, place = pair % 2, pair // 2
            y = pltpu.matmul_pop(y_acc[mxu][place])
            for half in range(2):
                slot = c * CHUNK + 2 * pair + half
                where = target(jnp.maximum(slot, 0))
                where = jnp.where(drop, NODE_SECTORS, where)
                ref = sums[2 * mxu + half]
                ref[where] = ref[where] + y[:, 128 * half : 128 * half + 128]

        for pair in range(PAIRS):
            mxu, place = pair % 2, pair // 2
            pltpu.matmul_pop(z_acc[mxu][place])
            pltpu.matmul_pop(y_acc[mxu][place])
        await_chunk(0)
        for pair in range(PAIRS):
            first_stage(0, pair)

        def turn(c, carry):
            await_chunk(c)
            waiting = []
            for place in range(DEPTH):
                for mxu in range(2):
                    pair = 2 * place + mxu
                    side = turned(pair)
                    first_stage(c, pair)
                    waiting.append((pair, side))
                if place >= 1:
                    for _ in range(2):
                        pair, side = waiting.pop(0)
                        add(c - 2, pair, c < 2)
                        second_stage(c - 1, pair, side)
            while waiting:
                pair, side = waiting.pop(0)
                add(c - 2, pair, c < 2)
                second_stage(c - 1, pair, side)
            return carry

        lax.fori_loop(1, chunks, turn, 0)
        for pair in range(PAIRS):
            side = turned(pair)
            add(chunks - 2, pair, chunks < 2)
            second_stage(chunks - 1, pair, side)
        for pair in range(PAIRS):
            add(chunks - 1, pair, False)

    accs = [[pltpu.ACC(mxu)((128, 256), jnp.float32) for _ in range(DEPTH)] for mxu in range(2)]
    pl.run_scoped(run, accs, accs)

    def finish(sector, carry):
        full = (sums_0[sector] + sums_1[sector]) + (sums_2[sector] + sums_3[sector])
        parts_ref[sector] = pack_rows(full)
        return carry

    lax.fori_loop(0, NODE_SECTORS, finish, 0)


def local_sums(env_blocks, iso_blocks, joined_sector, owner_map, live_pairs):
    pairs = env_blocks.shape[1]
    smem = pl.BlockSpec(memory_space=pltpu.SMEM)
    hbm = pl.BlockSpec(memory_space=pltpu.HBM)
    return pl.pallas_call(
        local_kernel,
        out_shape=(
            jax.ShapeDtypeStruct((NODE_SECTORS, ROWS, 128), jnp.float32),
            jax.ShapeDtypeStruct(owner_map.shape, jnp.int32),
        ),
        in_specs=[smem, smem, smem, hbm, hbm],
        out_specs=(pl.BlockSpec(memory_space=pltpu.VMEM), smem),
        scratch_shapes=[
            pltpu.VMEM((pairs, 128, 128), jnp.bfloat16),
            pltpu.VMEM((pairs, 128, 128), jnp.bfloat16),
            *[pltpu.VMEM((NODE_SECTORS + 1, 128, 128), jnp.float32)] * 4,
            pltpu.SemaphoreType.DMA((pairs // CHUNK,)),
            pltpu.SemaphoreType.DMA((pairs // CHUNK,)),
        ],
        name="local_sums",
    )(live_pairs, joined_sector, owner_map, env_blocks, iso_blocks)


def exchange_kernel(
    parts_ref, source_ref, out_ref,
    got_ref, own_ref, one_top, one_low, send_top, send_low, two_top, two_low,
    square_ref, square_one, square_sum, square_two,
    sent_sem, part_sem, top_one_sem, low_one_sem, top_two_sem, low_two_sem, square_one_sem, square_two_sem,
):
    me = lax.axis_index("sec")
    node = lax.axis_index("node")
    x, y, z = me // 16, (me // 4) % 4, me % 4
    near = y + 1 - 2 * (y % 2)
    far = (y + 3 + 2 * (y % 2)) % 4
    low = ROWS - TOP

    def plane(slot):
        dy, dz = slot // 4, slot % 4
        return x, (near if dy else y), (z + dz) % 4

    def column(slot):
        dy, dx = slot // 4, slot % 4
        return (x + dx) % 4, (far if dy else y), z

    def at(place, group=None):
        return (place[0] * 16 + place[1] * 4 + place[2], node if group is None else group)

    sends = []

    def send(src, dst, sem, device):
        copy = pltpu.make_async_remote_copy(
            src_ref=src, dst_ref=dst, send_sem=sent_sem.at[len(sends)], recv_sem=sem,
            device_id=device, device_id_type=MESH,
        )
        copy.start()
        sends.append(copy)
        return copy

    barrier = pltpu.get_barrier_semaphore()
    for slot in range(1, 8):
        pl.semaphore_signal(barrier, inc=1, device_id=at(plane(slot)), device_id_type=MESH)
        pl.semaphore_signal(barrier, inc=1, device_id=at(column(slot)), device_id_type=MESH)
    for slot in range(8):
        pl.semaphore_signal(barrier, inc=1, device_id=at(column(slot), 1 - node), device_id_type=MESH)
    pl.semaphore_wait(barrier, 22)

    part_copies = []
    for slot in range(1, 8):
        place = plane(slot)
        member = (place[1] % 2) * 4 + place[2]
        part_copies.append(
            send(parts_ref.at[member], got_ref.at[slot - 1], part_sem.at[slot - 1], at(place))
        )

    def cut(source):
        return source // 16, (source // 4) % 4, source % 4

    top_pick, low_pick = [], []
    for slot in range(8):
        xs, ys, zs = cut(source_ref[0, at(plane(slot))[0]])
        top_pick.append(jnp.where(ys == y, 0, 4) + (x + 4 - xs) % 4)
        xs, ys, zs = cut(source_ref[0, at(column(slot))[0]])
        low_pick.append(jnp.where(ys == y, 0, 4) + (z + 4 - zs) % 4)
    xs, ys, zs = cut(source_ref[0, me])
    far_s = (ys + 3 + 2 * (ys % 2)) % 4
    same = (y // 2) == (ys // 2)
    middle = jnp.where(same, ys, far_s)
    top_take = jnp.where(middle == y, 0, 4) + (z + 4 - zs) % 4
    low_take = jnp.where(same, 0, 4) + (x + 4 - xs) % 4

    row = lax.broadcasted_iota(jnp.int32, (128, 128), 0)
    lane = lax.broadcasted_iota(jnp.int32, (128, 128), 1)

    total = parts_ref[(y % 2) * 4 + z]
    for slot in range(1, 8):
        part_copies[slot - 1].wait_recv()
        total = total + got_ref[slot - 1]
    own_ref[...] = total
    one_top[0] = total[:TOP]
    one_low[0] = total[TOP:]

    top_copies, low_copies = [], []
    for slot in range(1, 8):
        top_copies.append(
            send(own_ref.at[pl.ds(0, TOP)], one_top.at[slot], top_one_sem.at[slot - 1], at(column(slot)))
        )
        low_copies.append(
            send(own_ref.at[pl.ds(TOP, low)], one_low.at[slot], low_one_sem.at[slot - 1], at(plane(slot)))
        )

    full = unpack_rows(total)
    weighed = jnp.where(row > lane, 2.0 * (full * full), jnp.where(row == lane, full * full, 0.0))
    squares = jnp.sum(weighed.reshape(16, 8, 128), axis=0)
    square_ref[...] = squares
    square_copies = []
    for index in range(1, 16):
        group = node if index < 8 else 1 - node
        square_copies.append(
            send(square_ref, square_one.at[index - 1], square_one_sem.at[index - 1], at(column(index % 8), group))
        )
    for index in range(1, 16):
        square_copies[index - 1].wait_recv()
        squares = squares + square_one[index - 1]
    square_sum[...] = squares
    square_copies = []
    for slot in range(1, 8):
        square_copies.append(
            send(square_sum, square_two.at[slot - 1], square_two_sem.at[slot - 1], at(plane(slot)))
        )

    for copy in top_copies:
        copy.wait_recv()
    for slot in range(1, 8):
        send_top[slot - 1] = one_top[top_pick[slot]]
    two_top[0] = one_top[top_pick[0]]
    top_copies = []
    for slot in range(1, 8):
        top_copies.append(
            send(send_top.at[slot - 1], two_top.at[slot], top_two_sem.at[slot - 1], at(plane(slot)))
        )
    for copy in low_copies:
        copy.wait_recv()
    for slot in range(1, 8):
        send_low[slot - 1] = one_low[low_pick[slot]]
    two_low[0] = one_low[low_pick[0]]
    low_copies = []
    for slot in range(1, 8):
        low_copies.append(
            send(send_low.at[slot - 1], two_low.at[slot], low_two_sem.at[slot - 1], at(column(slot)))
        )

    for slot in range(1, 8):
        square_copies[slot - 1].wait_recv()
        squares = squares + square_two[slot - 1]
    entries = 2 * 64 * 128 * 128
    factor = lax.rsqrt(jnp.sum(squares, keepdims=True) / entries + 1e-06)

    for copy in top_copies + low_copies:
        copy.wait_recv()
    full = unpack_rows(jnp.concatenate((two_top[top_take], two_low[low_take]), axis=0)) * factor
    lower = jnp.where(row >= lane, full, 0.0)
    out_ref[0, 0] = jnp.where(row >= lane, full, lower.T)

    for copy in sends:
        copy.wait_send()


def exchange(parts, source):
    low = ROWS - TOP
    f32 = jnp.float32
    dma = pltpu.SemaphoreType.DMA
    return pl.pallas_call(
        exchange_kernel,
        out_shape=jax.ShapeDtypeStruct((1, 1, 128, 128), f32),
        in_specs=[pl.BlockSpec(memory_space=pltpu.VMEM), pl.BlockSpec(memory_space=pltpu.SMEM)],
        out_specs=pl.BlockSpec(memory_space=pltpu.VMEM),
        scratch_shapes=[
            pltpu.VMEM((7, ROWS, 128), f32),
            pltpu.VMEM((ROWS, 128), f32),
            pltpu.VMEM((8, TOP, 128), f32),
            pltpu.VMEM((8, low, 128), f32),
            pltpu.VMEM((7, TOP, 128), f32),
            pltpu.VMEM((7, low, 128), f32),
            pltpu.VMEM((8, TOP, 128), f32),
            pltpu.VMEM((8, low, 128), f32),
            pltpu.VMEM((8, 128), f32),
            pltpu.VMEM((15, 8, 128), f32),
            pltpu.VMEM((8, 128), f32),
            pltpu.VMEM((7, 8, 128), f32),
            dma((57,)),
            dma((7,)), dma((7,)), dma((7,)), dma((7,)), dma((7,)), dma((15,)), dma((7,)),
        ],
        compiler_params=pltpu.CompilerParams(collective_id=0, has_side_effects=True),
        name="exchange",
    )(parts, source)


def body(env_blocks, iso_blocks, joined_sector, owner_map, live_pairs):
    parts, source = local_sums(env_blocks, iso_blocks, joined_sector, owner_map, live_pairs)
    return exchange(parts, source)


def solution(mesh):
    placed = (
        P("node", "sec", None, None),
        P("node", "sec", None, None),
        P("node", "sec"),
        P("node", None),
        P("node", "sec"),
    )
    return jax.shard_map(
        body, mesh=mesh, in_specs=placed, out_specs=P("node", "sec", None, None), check_vma=False
    )
```

time: 256 us -> 41.2 us (0.16)
  matrix products: 119 us -> 0 us
  blocking collectives: 97 us -> 0 us
  Pallas kernels: 0 us -> 38.9 us
  local copies, waits for them, and re-layouts: 27.1 us -> 1.47 us
  other arithmetic: 10 us -> 0 us
    dot_general x24 -> x0, matrix products: 119 us -> none  [the longest x12 87.8 us: add_group(): lax.dot_general(selector, flat_terms, (((0,), (0,)), ((), ())), precision...]
    all_to_all x1 -> x0, blocking collectives: 62.3 us -> none  [sum_at_owner(): lax.all_to_all(cut_along(shard, dim, length), axis, 0, 0, tiled=True)]
    pallas_call x0 -> x2, Pallas kernels: none -> 38.9 us  [the longest x1 29.2 us: exchange(): pl.pallas_call(exchange_kernel, out_shape=jax.ShapeDtypeStruct((1, 1, 128...]
    psum x4 -> x0, blocking collectives: 34.7 us -> none  [by_axis(): shard = lax.psum(shard, axis)]
    unnamed x6 -> x1, local copies, waits for them, and re-layouts: 13.7 us -> 1.47 us
    reshape x1 -> x0, local copies, waits for them, and re-layouts: 6.38 us -> none  [cut_along(): shard.reshape(*shape[:dim], length, shape[dim] // length, *shape[dim + 1:])]
    slice x4 -> x0, local copies, waits for them, and re-layouts: 4.06 us -> none  [the longest x1 3.8 us: body(): upper_left = partial_value[:, :half_width, :half_width]]
    reduce_sum x3 -> x0, other arithmetic: 3.93 us -> none  [the longest x1 2.48 us: sum_at_owner(): return jnp.sum(blocks, axis=0)]
where the time goes in v1:
time: 41.2 us; the launch traced here: 41 us
  Pallas kernels  38.9 us (94%)
  local copies, waits for them, and re-layouts  1.47 us (4%)
  between operations  0.67 us (2%)
    pallas_call x1, Pallas kernels, exchange(): pl.pallas_call(exchange_kernel, out_shape=jax.ShapeDtypeStruct((1, 1, 128...  29.2 us
    pallas_call x1, Pallas kernels, local_sums(): pl.pallas_call(local_kernel, out_shape=(jax.ShapeDtypeStruct((NODE_SECTOR...  9.6 us
    unnamed x1, local copies, waits for them, and re-layouts  1.47 us

profile of v1, /device:TPU:1, one launch (start us, length us, event | category | flops | bytes accessed | tf_op | source)
XLA Modules:
  0.0 41.0 jit_solution(12817045920794811645)
XLA Ops:
  0.7 9.6 %local_sums.1 = (f32[8,72,128]{2,1,0:T(8,128)}, s32[1,64]{1,0:T(1,128)}) custom-call(s32[1,1]{1,0:T(1,128)S(6)} %copy.7.live_ref, s32[1,384]{1,0:T(1,128)} %sector_ref.1, s32[1,64]{1,0:T(1,128)} %owner_ref.1, bf16[1,384,128,128]{3,2,1,0:T(8,128)(2,1)} %env_ref.1, bf16[1,384,128,128]{3,2,1,0:T(8,128)(2,1)} %iso_ref.1), custom_call_target="tpu_custom_call" | custom-call | tf_op jit(solution)/shard_map/local_sums/pallas_call | solution.py:173
  10.3 29.2 %exchange.1 = f32[1,1,128,128]{3,2,1,0:T(8,128)} custom-call(f32[8,72,128]{2,1,0:T(8,128)} %get-tuple-element.7.parts_ref, s32[1,64]{1,0:T(1,128)} %get-tuple-element.8.source_ref), custom_call_target="tpu_custom_call" | custom-call | tf_op jit(solution)/shard_map/exchange/pallas_call | solution.py:340
  39.5 1.5 %copy.8 = f32[1,1,128,128]{3,2,1,0:T(8,128)} copy(f32[1,1,128,128]{3,2,1,0:T(8,128)} %exchange.1) | data formatting | bytes 131072

commit v2 on v1

v2 whole, which is shorter than its diff:
```python
import functools

import jax
import jax.numpy as jnp
from jax import lax
from jax.experimental import pallas as pl
from jax.experimental.pallas import tpu as pltpu
from jax.sharding import PartitionSpec as P

MESH = pl.DeviceIdType.MESH
NODE_SECTORS = 8
CHUNK = 16
PAIRS = CHUNK // 2
DEPTH = PAIRS // 2
ROWS = 72
TOP = 40


def pack_rows(full):
    lane = lax.broadcasted_iota(jnp.int32, (16, 128), 1)
    rows = [full[112:128]]
    for low in range(3):
        high = 6 - low
        width = 16 * (high + 1)
        short = pltpu.roll(full[16 * low : 16 * low + 16], width, 1)
        rows.append(jnp.where(lane < width, full[16 * high : 16 * high + 16], short))
    rows.append(jnp.where(lane[:8] < 64, full[48:56], pltpu.roll(full[56:64], 64, 1)))
    return jnp.concatenate(rows, axis=0)


def unpack_rows(packed):
    blocks = [None] * 8
    blocks[7] = packed[0:16]
    for low in range(3):
        high = 6 - low
        width = 16 * (high + 1)
        both = packed[16 + 16 * low : 32 + 16 * low]
        blocks[high] = both
        blocks[low] = pltpu.roll(both, 128 - width, 1)
    blocks[3] = jnp.concatenate((packed[64:72], pltpu.roll(packed[64:72], 64, 1)), axis=0)
    return jnp.concatenate(blocks, axis=0)


def local_kernel(
    live_ref, sector_hbm, owner_hbm, env_ref, iso_ref, parts_ref, source_ref,
    sector_ref, owner_ref, env_buf, iso_buf, carry_buf,
    sums_0, sums_1, sums_2, sums_3, env_sem, iso_sem, small_sem,
):
    slots = env_buf.shape[0]
    sums = (sums_0, sums_1, sums_2, sums_3)

    def copies(c):
        first = pl.multiple_of(c * CHUNK, CHUNK)
        span = pl.ds(first, CHUNK)
        return (
            pltpu.make_async_copy(iso_ref.at[0, span], iso_buf.at[span], iso_sem.at[c]),
            pltpu.make_async_copy(env_ref.at[0, span], env_buf.at[span], env_sem.at[c]),
        )

    def start(c, carry):
        for copy in copies(c):
            copy.start()
        return carry

    small = [
        pltpu.make_async_copy(src, dst, small_sem.at[i])
        for i, (src, dst) in enumerate(
            ((sector_hbm, sector_ref), (owner_hbm, owner_ref))
        )
    ]
    for copy in small:
        copy.start()
    lax.fori_loop(0, slots // CHUNK, start, 0)

    def clear(sector, carry):
        for ref in sums:
            ref[sector] = jnp.zeros((128, 128), jnp.float32)
        return carry

    lax.fori_loop(0, NODE_SECTORS + 1, clear, 0)
    for copy in small:
        copy.wait()
    live = live_ref[0, 0]
    doubles = (live + 2 * CHUNK - 1) // (2 * CHUNK)
    last = 2 * doubles - 1

    def invert(sector, carry):
        source_ref[0, owner_ref[0, sector]] = sector
        return carry

    lax.fori_loop(0, owner_ref.shape[1], invert, 0, unroll=8)

    def await_chunk(c):
        for copy in copies(c):
            copy.wait()

    def target(slot):
        counts = jnp.logical_and(slot >= 0, slot < live)
        return jnp.where(counts, lax.rem(sector_ref[0, jnp.maximum(slot, 0)], NODE_SECTORS), NODE_SECTORS)

    def stage(c, place, mxu, register):
        first = c * CHUNK + 2 * (2 * place + mxu)
        none = jnp.zeros((128, 128), jnp.bfloat16)
        top = jnp.concatenate((iso_buf[first], none), axis=1)
        bottom = jnp.concatenate((none, iso_buf[first + 1]), axis=1)
        pltpu.matmul_push_rhs(
            jnp.concatenate((top, bottom), axis=0), staging_register=register, mxu_index=mxu
        )

    def run(z_acc, y_acc):
        def turned(place, mxu):
            z = pltpu.matmul_pop(z_acc[mxu][place]).astype(jnp.bfloat16)
            return jnp.concatenate((z[:, :128].T, z[:, 128:].T), axis=1)

        def first_stage(c, place, mxu, register):
            stage(c, place, mxu, register)
            first = c * CHUNK + 2 * (2 * place + mxu)
            side = jnp.concatenate((env_buf[first], env_buf[first + 1]), axis=1)
            pltpu.matmul_acc_lhs(z_acc[mxu][place], side, load_staged_rhs=register)

        def add(c, place, mxu):
            y = pltpu.matmul_pop(y_acc[mxu][place])
            for half in range(2):
                where = target(c * CHUNK + 2 * (2 * place + mxu) + half)
                ref = sums[2 * mxu + half]
                ref[where] = ref[where] + y[:, 128 * half : 128 * half + 128]

        def second_stage(place, mxu, register, side):
            pltpu.matmul_acc_lhs(y_acc[mxu][place], side, load_staged_rhs=register)

        both = range(2)

        def turn(c, sides):
            for mxu in both:
                add(c - 3, 3, mxu)
                second_stage(3, mxu, 0, sides[mxu])
            turns = []
            for place in range(2):
                turns.append([turned(place, mxu) for mxu in both])
                for mxu in both:
                    first_stage(c, place, mxu, 1 - place)
            for mxu in both:
                add(c - 2, 0, mxu)
                stage(c - 1, 0, mxu, 1)
                second_stage(0, mxu, 1, turns[0][mxu])
            for place in range(2, 4):
                turns.append([turned(place, mxu) for mxu in both])
                for mxu in both:
                    first_stage(c, place, mxu, 0)
                for mxu in both:
                    add(c - 2, place - 1, mxu)
                    stage(c - 1, place - 1, mxu, 1)
                    second_stage(place - 1, mxu, 1, turns[place - 1][mxu])
            for mxu in both:
                stage(c - 1, 3, mxu, 0)
            return turns[3]

        for place in range(DEPTH):
            for mxu in both:
                pltpu.matmul_pop(z_acc[mxu][place])
                pltpu.matmul_pop(y_acc[mxu][place])
        await_chunk(0)
        for place in range(DEPTH):
            for mxu in both:
                first_stage(0, place, mxu, place % 2)
        for mxu in both:
            stage(0, 3, mxu, 0)
            carry_buf[mxu] = jnp.zeros((128, 256), jnp.bfloat16)

        def double(step, carry):
            c = 2 * step + 1
            await_chunk(c)
            await_chunk(c + 1)
            sides = turn(c, [carry_buf[mxu] for mxu in both])
            sides = turn(c + 1, sides)
            for mxu in both:
                carry_buf[mxu] = sides[mxu]
            return carry

        lax.fori_loop(0, doubles - 1, double, 0)
        await_chunk(last)
        sides = turn(last, [carry_buf[mxu] for mxu in both])
        turns = [[turned(place, mxu) for mxu in both] for place in range(2)]
        for mxu in both:
            add(last - 2, 3, mxu)
            second_stage(3, mxu, 0, sides[mxu])
        for place in range(2, 4):
            turns.append([turned(place, mxu) for mxu in both])
        for place in range(4):
            for mxu in both:
                add(last - 1, place, mxu)
                stage(last, place, mxu, 1 - place % 2)
                second_stage(place, mxu, 1 - place % 2, turns[place][mxu])
        for place in range(4):
            for mxu in both:
                add(last, place, mxu)

    accs = [[pltpu.ACC(mxu)((128, 256), jnp.float32) for _ in range(DEPTH)] for mxu in range(2)]
    pl.run_scoped(run, accs, accs)

    for sector in range(NODE_SECTORS):
        full = (sums_0[sector] + sums_1[sector]) + (sums_2[sector] + sums_3[sector])
        parts_ref[sector] = pack_rows(full)

    def rest(c, carry):
        await_chunk(c)
        return carry

    lax.fori_loop(last + 1, slots // CHUNK, rest, 0)


def local_sums(env_blocks, iso_blocks, joined_sector, owner_map, live_pairs):
    pairs = env_blocks.shape[1]
    hbm = pl.BlockSpec(memory_space=pltpu.HBM)
    return pl.pallas_call(
        local_kernel,
        out_shape=(
            pltpu.VMEM((NODE_SECTORS, ROWS, 128), jnp.float32),
            pltpu.SMEM(owner_map.shape, jnp.int32),
        ),
        in_specs=[pl.BlockSpec(memory_space=pltpu.SMEM)] + [hbm] * 4,
        out_specs=(pl.BlockSpec(memory_space=pltpu.VMEM), pl.BlockSpec(memory_space=pltpu.SMEM)),
        scratch_shapes=[
            pltpu.SMEM(joined_sector.shape, jnp.int32),
            pltpu.SMEM(owner_map.shape, jnp.int32),
            pltpu.VMEM((pairs, 128, 128), jnp.bfloat16),
            pltpu.VMEM((pairs, 128, 128), jnp.bfloat16),
            pltpu.VMEM((2, 128, 256), jnp.bfloat16),
            *[pltpu.VMEM((NODE_SECTORS + 1, 128, 128), jnp.float32)] * 4,
            pltpu.SemaphoreType.DMA((pairs // CHUNK,)),
            pltpu.SemaphoreType.DMA((pairs // CHUNK,)),
            pltpu.SemaphoreType.DMA((2,)),
        ],
        compiler_params=pltpu.CompilerParams(vmem_limit_bytes=40 * 2**20),
        name="local_sums",
    )(live_pairs, *[
        pltpu.with_memory_space_constraint(array, pltpu.HBM)
        for array in (joined_sector, owner_map, env_blocks, iso_blocks)
    ])


def exchange_kernel(
    parts_ref, source_ref, rows_ref, squares_ref,
    got_ref, own_ref, one_top, one_low, send_top, send_low, two_top, two_low,
    square_own, square_one, square_group, square_side, square_both, square_two, sent_sem, got_sem,
):
    me = lax.axis_index("sec")
    node = lax.axis_index("node")
    x, y, z = me // 16, (me // 4) % 4, me % 4
    near = y + 1 - 2 * (y % 2)
    far = (y + 3 + 2 * (y % 2)) % 4
    low = ROWS - TOP
    order = (6, 2, 5, 7, 1, 3, 4)

    def plane(slot):
        dy, dz = slot // 4, slot % 4
        return x * 16 + (near if dy else y) * 4 + (z + dz) % 4

    def column(slot):
        dy, dx = slot // 4, slot % 4
        return (x + dx) % 4 * 16 + (far if dy else y) * 4 + z

    def send(src, dst, phase, place, group=node):
        pltpu.make_async_remote_copy(
            src_ref=src, dst_ref=dst, send_sem=sent_sem.at[phase], recv_sem=got_sem.at[phase],
            device_id=(place, group), device_id_type=MESH,
        ).start()

    def landed(ref, phase):
        pltpu.make_async_copy(ref, ref, got_sem.at[phase]).wait()

    def left(ref, phase):
        pltpu.make_async_copy(ref, ref, sent_sem.at[phase]).wait()

    barrier = pltpu.get_barrier_semaphore()
    for slot in order:
        pl.semaphore_signal(barrier, inc=1, device_id=(plane(slot), node), device_id_type=MESH)
    for slot in order:
        pl.semaphore_signal(barrier, inc=1, device_id=(column(slot), node), device_id_type=MESH)
    pl.semaphore_signal(barrier, inc=1, device_id=(me, 1 - node), device_id_type=MESH)
    pl.semaphore_wait(barrier, 15)

    for slot in order:
        member = plane(slot) % 8
        send(parts_ref.at[member], got_ref.at[slot - 1], 0, plane(slot))

    def cut(source):
        return source // 16, (source // 4) % 4, source % 4

    top_pick, low_pick = [], []
    for slot in range(8):
        xs, ys, zs = cut(source_ref[0, plane(slot)])
        top_pick.append(jnp.where(ys == y, 0, 4) + (x + 4 - xs) % 4)
        xs, ys, zs = cut(source_ref[0, column(slot)])
        low_pick.append(jnp.where(ys == y, 0, 4) + (z + 4 - zs) % 4)
    xs, ys, zs = cut(source_ref[0, me])
    far_s = (ys + 3 + 2 * (ys % 2)) % 4
    same = (y // 2) == (ys // 2)
    middle = jnp.where(same, ys, far_s)
    top_take = jnp.where(middle == y, 0, 4) + (z + 4 - zs) % 4
    low_take = jnp.where(same, 0, 4) + (x + 4 - xs) % 4

    row = lax.broadcasted_iota(jnp.int32, (128, 128), 0)
    lane = lax.broadcasted_iota(jnp.int32, (128, 128), 1)

    total = parts_ref[me % 8]
    landed(got_ref, 0)
    for slot in range(7):
        total = total + got_ref[slot]
    own_ref[...] = total
    one_top[0] = total[:TOP]
    one_low[0] = total[TOP:]

    for slot in order:
        send(own_ref.at[pl.ds(TOP, low)], one_low.at[slot], 1, plane(slot))
    full = unpack_rows(total)
    squared = full * full
    weighed = jnp.where(row > lane, squared + squared, jnp.where(row == lane, squared, 0.0))
    squares = jnp.sum(weighed.reshape(16, 8, 128), axis=0)
    square_own[...] = squares
    for slot in order:
        send(square_own, square_one.at[slot - 1], 2, column(slot))
    for slot in order:
        send(own_ref.at[pl.ds(0, TOP)], one_top.at[slot], 3, column(slot))
    landed(square_one, 2)
    for slot in range(7):
        squares = squares + square_one[slot]
    square_group[...] = squares
    send(square_group, square_side, 4, me, 1 - node)

    landed(one_low.at[pl.ds(1, 7)], 1)
    for slot in range(1, 8):
        send_low[slot - 1] = one_low[low_pick[slot]]
    two_low[0] = one_low[low_pick[0]]
    for slot in order:
        send(send_low.at[slot - 1], two_low.at[slot], 5, column(slot))
    landed(square_side, 4)
    squares = squares + square_side[...]
    square_both[...] = squares
    for slot in order:
        send(square_both, square_two.at[slot - 1], 6, plane(slot))
    landed(one_top.at[pl.ds(1, 7)], 3)
    for slot in range(1, 8):
        send_top[slot - 1] = one_top[top_pick[slot]]
    two_top[0] = one_top[top_pick[0]]
    for slot in order:
        send(send_top.at[slot - 1], two_top.at[slot], 7, plane(slot))

    landed(square_two, 6)
    for slot in range(7):
        squares = squares + square_two[slot]
    squares_ref[...] = squares
    left(got_ref, 0)
    left(send_low, 1)
    left(square_one, 2)
    left(send_top, 3)
    left(square_side, 4)
    left(square_two, 6)
    landed(two_low.at[pl.ds(1, 7)], 5)
    rows_ref[pl.ds(TOP, low)] = two_low[low_take]
    landed(two_top.at[pl.ds(1, 7)], 7)
    rows_ref[pl.ds(0, TOP)] = two_top[top_take]
    left(send_low, 5)
    left(send_top, 7)


def exchange(parts, source):
    low = ROWS - TOP
    f32 = jnp.float32
    vmem = pl.BlockSpec(memory_space=pltpu.VMEM)
    return pl.pallas_call(
        exchange_kernel,
        out_shape=(pltpu.VMEM((ROWS, 128), f32), pltpu.VMEM((8, 128), f32)),
        in_specs=[vmem, pl.BlockSpec(memory_space=pltpu.SMEM)],
        out_specs=(vmem, vmem),
        scratch_shapes=[
            pltpu.VMEM((7, ROWS, 128), f32),
            pltpu.VMEM((ROWS, 128), f32),
            pltpu.VMEM((8, TOP, 128), f32),
            pltpu.VMEM((8, low, 128), f32),
            pltpu.VMEM((7, TOP, 128), f32),
            pltpu.VMEM((7, low, 128), f32),
            pltpu.VMEM((8, TOP, 128), f32),
            pltpu.VMEM((8, low, 128), f32),
            pltpu.VMEM((8, 128), f32),
            pltpu.VMEM((7, 8, 128), f32),
            pltpu.VMEM((8, 128), f32),
            pltpu.VMEM((8, 128), f32),
            pltpu.VMEM((8, 128), f32),
            pltpu.VMEM((7, 8, 128), f32),
            pltpu.SemaphoreType.DMA((8,)),
            pltpu.SemaphoreType.DMA((8,)),
        ],
        compiler_params=pltpu.CompilerParams(
            collective_id=0, has_side_effects=True, vmem_limit_bytes=8 * 2**20
        ),
        name="exchange",
    )(
        pltpu.with_memory_space_constraint(parts, pltpu.VMEM),
        pltpu.with_memory_space_constraint(source, pltpu.SMEM),
    )


def finish_kernel(rows_ref, squares_ref, out_ref):
    row = lax.broadcasted_iota(jnp.int32, (128, 128), 0)
    lane = lax.broadcasted_iota(jnp.int32, (128, 128), 1)
    entries = 2 * 64 * 128 * 128
    factor = lax.rsqrt(jnp.sum(squares_ref[...], keepdims=True) / entries + 1e-06)
    full = unpack_rows(rows_ref[...])
    lower = jnp.where(row >= lane, full, 0.0)
    out_ref[0, 0] = jnp.where(row >= lane, full, lower.T) * factor


def finish(rows, squares):
    vmem = pl.BlockSpec(memory_space=pltpu.VMEM)
    return pl.pallas_call(
        finish_kernel,
        out_shape=jax.ShapeDtypeStruct((1, 1, 128, 128), jnp.float32),
        in_specs=[vmem, vmem],
        out_specs=vmem,
        compiler_params=pltpu.CompilerParams(vmem_limit_bytes=8 * 2**20),
        name="finish",
    )(
        pltpu.with_memory_space_constraint(rows, pltpu.VMEM),
        pltpu.with_memory_space_constraint(squares, pltpu.VMEM),
    )


def body(env_blocks, iso_blocks, joined_sector, owner_map, live_pairs):
    parts, source = local_sums(env_blocks, iso_blocks, joined_sector, owner_map, live_pairs)
    return finish(*exchange(parts, source))


def solution(mesh):
    placed = (
        P("node", "sec", None, None),
        P("node", "sec", None, None),
        P("node", "sec"),
        P("node", None),
        P("node", "sec"),
    )
    return jax.shard_map(
        body, mesh=mesh, in_specs=placed, out_specs=P("node", "sec", None, None), check_vma=False
    )
```

time: 41.2 us -> 34 us (0.83)
  Pallas kernels: 38.9 us -> 33.2 us
  local copies, waits for them, and re-layouts: 1.47 us -> 0 us
    pallas_call x2 -> x3, Pallas kernels: 38.9 us -> 33.2 us  [the longest x1 23.7 us: exchange(): pl.pallas_call(exchange_kernel, out_shape=(pltpu.VMEM((ROWS, 128), f32),...]
    unnamed x1 -> x0, local copies, waits for them, and re-layouts: 1.47 us -> none
where the time goes in v2:
time: 34 us; the launch traced here: 33.8 us
  Pallas kernels  33.2 us (98%)
  between operations  0.67 us (2%)
    pallas_call x1, Pallas kernels, exchange(): pl.pallas_call(exchange_kernel, out_shape=(pltpu.VMEM((ROWS, 128), f32),...  23.7 us
    pallas_call x1, Pallas kernels, local_sums(): pl.pallas_call(local_kernel, out_shape=(pltpu.VMEM((NODE_SECTORS, ROWS, 1...  8.64 us
    pallas_call x1, Pallas kernels, finish(): pl.pallas_call(finish_kernel, out_shape=jax.ShapeDtypeStruct((1, 1, 128,...  0.81 us

profile of v2, /device:TPU:1, one launch (start us, length us, event | category | flops | bytes accessed | tf_op | source)
XLA Modules:
  0.0 33.8 jit_solution(8490953720607463887)
XLA Ops:
  0.7 8.6 %local_sums.1 = (f32[8,72,128]{2,1,0:T(8,128)S(1)}, s32[1,64]{1,0:T(1,128)S(4)}) custom-call(s32[1,1]{1,0:T(1,128)S(6)} %copy.6.live_ref, s32[1,384]{1,0:T(1,128)} %sector_hbm.1, s32[1,64]{1,0:T(1,128)} %owner_hbm.1, bf16[1,384,128,128]{3,2,1,0:T(8,128)(2,1)} %env_ref.1, bf16[1,384,128,128]{3,2,1,0:T(8,128)(2,1)} %iso_ref.1), custom_call_target="tpu_custom_call" | custom-call | tf_op jit(solution)/shard_map/local_sums/pallas_call | solution.py:215
  9.3 23.7 %exchange.1 = (f32[72,128]{1,0:T(8,128)S(1)}, f32[8,128]{1,0:T(8,128)S(1)}) custom-call(f32[8,72,128]{2,1,0:T(8,128)S(1)} %get-tuple-element.9.parts_ref, s32[1,64]{1,0:T(1,128)S(4)} %get-tuple-element.10.source_ref), custom_call_target="tpu_custom_call" | custom-call | tf_op jit(solution)/shard_map/exchange/pallas_call | solution.py:371
  33.0 0.8 %finish.1 = f32[1,1,128,128]{3,2,1,0:T(8,128)} custom-call(f32[72,128]{1,0:T(8,128)S(1)} %get-tuple-element.11.rows_ref, f32[8,128]{1,0:T(8,128)S(1)} %get-tuple-element.12.squares_ref), custom_call_target="tpu_custom_call" | custom-call | tf_op jit(solution)/shard_map/finish/pallas_call | solution.py:416
